TPU v7x, 32 devices: a whole 2x2x4 slice. The times are simulated.
32 devices in a mesh: gx: 8 (over z, x), gy: 4 (over y, core).
Axes of the slice: x: 2, y: 2, z: 4, core: 2. Of those that a mesh axis runs over, the one named last changes fastest.
Arguments:
- gradient: float32 [1024, 128], P('gx', 'gy'), may hold values from -6 to 6
- stat_old: float32 [1024, 1024], P('gx', 'gy'), may hold values from -1.001 to 1.001, as said below
Outputs:
- statistic: float32 [1024, 1024], P('gx', 'gy')
- inverse_root: float32 [1024, 1024], P('gx', 'gy')
Inputs may be any that keep to these rules, and one draw needn't show every extreme that they name: stat_old is symmetric positive semidefinite with unit diagonal, the Gram matrix of 1024 unit-length rows of 256 entries.
All inputs are finite; a program needn't handle non-finite values.
Results may differ from a plain program's by a relative error of at most 0.0003.
Values sent between devices are 32-bit elements.
A program may use at most 64 MiB of HBM per device.

v0:
```python
import jax
import jax.numpy as jnp
from jax import lax
from jax.sharding import PartitionSpec as P


def folded(shard, axis, dim, absorb, state):
    everything = jax.tree.map(lambda a: lax.all_gather(a, axis, axis=dim, tiled=True), shard)
    return absorb(state, everything, jnp.int32(0))


def spread(block, axis, owner):
    block = jnp.where(lax.axis_index(axis) == owner, block, jnp.zeros_like(block))
    return lax.psum(block, axis)


def matmul(leading, trailing):
    return jnp.dot(
        leading, trailing, preferred_element_type=jnp.float32, precision=lax.Precision.HIGHEST
    )


def panels(factor_one, factor_two):
    whole_row = lax.all_gather(factor_one, "gy", axis=1, tiled=True)

    def accumulate(running, shard_rows, first_row):
        matching = lax.dynamic_slice_in_dim(whole_row, first_row, shard_rows.shape[0], 1)
        return running + matmul(matching, shard_rows)

    empty = jnp.zeros((factor_one.shape[0], factor_two.shape[1]), jnp.float32)
    return folded(factor_two, "gx", 0, accumulate, empty)


def product(factor_one, factor_two):
    return panels(factor_one, factor_two)


def local(gradient, stat_old):
    count_rows = lax.axis_size("gx")
    count_cols = lax.axis_size("gy")
    factor = count_rows // count_cols
    piece_width = stat_old.shape[0]
    row_index = lax.axis_index("gx")
    col_index = lax.axis_index("gy")
    panel_rows = lax.all_gather(gradient, "gy", axis=1, tiled=True)
    outer_parts = []
    for member in range(factor):
        column_rows = spread(panel_rows, "gx", col_index * factor + member)
        outer_parts.append(matmul(panel_rows, column_rows.T))
    outer = jnp.concatenate(outer_parts, axis=1) / panel_rows.shape[1]
    statistic = 0.9 * stat_old + outer
    squares = lax.psum(jnp.sum(statistic * statistic), ("gx", "gy"))
    divisor = 2.0 * jnp.sqrt(squares / (piece_width * count_rows))
    global_rows = row_index * piece_width + lax.broadcasted_iota(jnp.int32, stat_old.shape, 0)
    global_cols = col_index * (factor * piece_width) + lax.broadcasted_iota(
        jnp.int32, stat_old.shape, 1
    )
    identity = (global_rows == global_cols).astype(jnp.float32)
    normed = statistic / divisor
    first_step = 1.5 * identity - 0.5 * normed
    root_half = product(normed, first_step)
    product_mid = product(first_step, root_half)
    second_step = 1.5 * identity - 0.5 * product_mid
    inverse_root = product(second_step, first_step)
    return (statistic, inverse_root)


def solution(mesh):
    return jax.shard_map(
        local,
        mesh=mesh,
        in_specs=(P("gx", "gy"), P("gx", "gy")),
        out_specs=(P("gx", "gy"), P("gx", "gy")),
        check_vma=False,
    )
```

profile of v0, /device:TPU:3, one launch (start us, length us, event | category | flops | bytes accessed | tf_op | source)
XLA Modules:
  0.0 229.4 jit_solution(9310152714000626148)
XLA Ops:
  7.2 0.0 all-reduce.3.cloned.1.call-start
  7.2 0.6 copy-done.4
  7.9 5.7 %all_gather.19 = f32[128,128]{0,1:T(8,128)S(1)} all-gather(f32[128,32]{0,1:T(8,128)S(1)} %copy-done.4), channel_id=1, replica_groups=mesh['gx'=8,'gy'=4] {'gy'}, dimensions={1}, use_global_device_ids=true | all-gather | bytes 81920 | tf_op jit(solution)/shard_map/all_gather | solution.py:45
  13.6 0.7 broadcast_select_fusion.1
  14.3 0.0 all-gather.3.cloned.1.call-start
  14.4 0.2 copy-done.2
  14.6 0.1 copy.4
  14.7 68.3 %all-reduce.3.cloned.1.call-done = (f32[128,128]{0,1:T(8,128)}, f32[128,128]{0,1:T(8,128)}) async-done(((f32[128,128]{0,1:T(8,128)}, f32[128,128]{0,1:T(8,128)}), (f32[128,128]{0,1:T(8,128)}, f32[128,128]{0,1:T(8,128)})) %all-reduce.3.cloned.1.call-update) | async-done | bytes 131088 | tf_op jit(solution)/shard_map/psum | solution.py:14
  83.0 1.2 convolution_bitcast_fusion
  84.2 0.3 convolution_bitcast_fusion.1
  84.5 0.6 multiply_reduce_fusion
  85.1 41.7 %psum.23 = f32[]{:T(128)} all-reduce(f32[]{:T(128)} %get-tuple-element.8), channel_id=1, replica_groups=mesh['gx'=8,'gy'=4] {'gx','gy'}, use_global_device_ids=true, to_apply=%region_3.4 | all-reduce | flops 1 | bytes 8 | tf_op jit(solution)/shard_map/psum | solution.py:52
  127.6 0.8 select_subtract_fusion
  128.3 0.0 all-gather.5.cloned.1.call-start
  128.4 8.6 %all_gather.21 = f32[128,1024]{0,1:T(8,128)S(1)} all-gather(f32[128,256]{0,1:T(8,128)S(1)} %get-tuple-element.7), channel_id=1, replica_groups=mesh['gx'=8,'gy'=4] {'gy'}, dimensions={1}, use_global_device_ids=true | all-gather | bytes 655360 | tf_op jit(solution)/shard_map/all_gather | solution.py:24
  137.0 29.3 %all-gather.3.cloned.1.call-done = f32[1024,256]{0,1:T(8,128)} async-done(((f32[128,256]{0,1:T(8,128)}), f32[1024,256]{0,1:T(8,128)}) %all-gather.3.cloned.1.call-update) | async-done | bytes 1048592 | tf_op jit(solution)/shard_map/all_gather | solution.py:8
  166.2 2.9 %fusion.3 = f32[128,256]{1,0:T(8,128)} fusion(f32[128,1024]{0,1:T(8,128)S(1)} %all_gather.21, f32[1024,256]{0,1:T(8,128)} %all-gather.3.cloned.1.call-done), kind=kOutput, calls=%fused_computation.13 | convolution fusion | flops 402653184 | bytes 1703936 | tf_op jit(solution)/shard_map/dot_general | solution.py:18
  169.1 0.8 copy.5
  169.9 0.1 copy-done.1
  170.0 9.4 %all_gather.20 = f32[128,1024]{0,1:T(8,128)S(1)} all-gather(f32[128,256]{0,1:T(8,128)S(1)} %copy-done.1), channel_id=1, replica_groups=mesh['gx'=8,'gy'=4] {'gy'}, dimensions={1}, use_global_device_ids=true | all-gather | bytes 655360 | tf_op jit(solution)/shard_map/all_gather | solution.py:24
  179.4 28.9 %all-gather.5.cloned.1.call-done = f32[1024,256]{1,0:T(8,128)} async-done(((f32[128,256]{1,0:T(8,128)}), f32[1024,256]{1,0:T(8,128)}) %all-gather.5.cloned.1.call-update) | async-done | bytes 1048592 | tf_op jit(solution)/shard_map/all_gather | solution.py:8
  208.4 3.0 %fusion = f32[128,256]{0,1:T(8,128)S(1)} fusion(f32[128,1024]{0,1:T(8,128)S(1)} %all_gather.20, f32[1024,256]{1,0:T(8,128)} %all-gather.5.cloned.1.call-done, s32[128]{0:T(128)S(1)} %iota_add_fusion.1, s32[256]{0:T(256)S(1)} %iota_add_fusion), kind=kOutput, calls=%fused_computation.1 | convolution fusion | flops 402784256 | bytes 1705472 | tf_op jit(solution)/shard_map/dot_general | solution.py:18
  211.4 9.8 %all_gather.24 = f32[128,1024]{0,1:T(8,128)S(1)} all-gather(f32[128,256]{0,1:T(8,128)S(1)} %fusion), channel_id=1, replica_groups=mesh['gx'=8,'gy'=4] {'gy'}, dimensions={1}, use_global_device_ids=true | all-gather | bytes 655360 | tf_op jit(solution)/shard_map/all_gather | solution.py:24
  221.2 1.7 fusion.4
  (12 shorter events, 0.1 us)
Async XLA Ops:
  7.2 0.7 copy-start.4
  7.2 75.8 %all-reduce.3.cloned.1.call-start = ((), (), s32[]{:S(2)}) async-start(), calls=%async_computation.2 | async-start | bytes 262144 | tf_op jit(solution)/shard_map/psum | solution.py:14
  13.6 1.0 copy-start.2
  14.3 151.9 %all-gather.3.cloned.1.call-start = ((), (), s32[]{:S(2)}) async-start(), calls=%async_computation | async-start | bytes 1179648 | tf_op jit(solution)/shard_map/all_gather | solution.py:8
  83.0 1.2 copy-start.3
  128.3 80.0 %all-gather.5.cloned.1.call-start = ((), (), s32[]{:S(2)}) async-start(), calls=%async_computation.1 | async-start | bytes 1179648 | tf_op jit(solution)/shard_map/all_gather | solution.py:8
  169.1 0.9 copy-start.1
  179.4 41.7 %copy-start = (f32[1024,256]{0,1:T(8,128)S(1)}, f32[1024,256]{0,1:T(8,128)}, u32[]{:S(2)}) copy-start(f32[1024,256]{0,1:T(8,128)} %all-gather.3.cloned.1.call-done) | copy-start | bytes 3145732
Sparse Core Ops, SparseCore 0:
  14.4 68.5 all-reduce.2
  128.5 37.7 all-gather.2
  169.2 39.0 all-gather.4
where the time goes:
time: 232 us; the launch traced here: 229 us
  waiting for transfers between devices  127 us (55%)
  blocking collectives  75.3 us (32%)
  between operations  14.5 us (6%)
  matrix products  9 us (4%)
    psum x1, waiting for transfers between devices, spread(): return lax.psum(block, axis)  68.3 us
    all_gather x2, waiting for transfers between devices, folded(): lax.all_gather(a, axis, axis=dim, tiled=True)  58.2 us
    psum x1, blocking collectives, local(): squares = lax.psum(jnp.sum(statistic * statistic), ('gx', 'gy'))  41.7 us
    all_gather x3, blocking collectives, panels(): whole_row = lax.all_gather(factor_one, 'gy', axis=1, tiled=True)  27.8 us
    dot_general x5, matrix products, matmul(): jnp.dot(leading, trailing, preferred_element_type=jnp.float32, precision=...  9 us
    all_gather x1, blocking collectives, local(): panel_rows = lax.all_gather(gradient, 'gy', axis=1, tiled=True)  5.73 us
  transfers between devices with their start and end apart: 3, of which 3 were waited for; matrix products, arithmetic and copies ran while one was open for 0% of the time, Pallas kernels for 0%

commit v1 on v0

v1 whole, which is shorter than its diff:
```python
import jax
import jax.numpy as jnp
from jax import lax
from jax.sharding import PartitionSpec as P


def matmul(leading, trailing, precision):
    return jnp.dot(leading, trailing, preferred_element_type=jnp.float32, precision=precision)


def whole(block):
    rows = lax.all_gather(block, "gy", axis=1, tiled=True)
    return lax.all_gather(rows, "gx", axis=0, tiled=True)


def local(gradient, stat_old):
    height, width = stat_old.shape
    row_start = lax.axis_index("gx") * height
    col_start = lax.axis_index("gy") * width
    grad = whole(gradient)
    stat = whole(stat_old)
    high = lax.Precision.HIGH
    full = 0.9 * stat + matmul(grad, grad.T, high) / grad.shape[1]
    side = full.shape[0]
    row_panel = lax.dynamic_slice_in_dim(full, row_start, height, 0)
    col_panel = lax.dynamic_slice_in_dim(full, col_start, width, 1)
    statistic = lax.dynamic_slice_in_dim(row_panel, col_start, width, 1)
    scale = 0.5 * lax.rsqrt(jnp.sum(full * full) / side)
    square_rows = matmul(row_panel, full, high)
    square_cols = matmul(full, col_panel, high)

    def eye(shape, first_row, first_col):
        rows = first_row + lax.broadcasted_iota(jnp.int32, shape, 0)
        cols = first_col + lax.broadcasted_iota(jnp.int32, shape, 1)
        return (rows == cols).astype(jnp.float32)

    def quad(square, panel, first_row, first_col):
        ident = eye(square.shape, first_row, first_col)
        return (0.25 * scale * scale) * square - (1.125 * scale) * panel + 0.84375 * ident

    left = quad(square_rows, row_panel, row_start, 0)
    right = quad(square_cols, col_panel, 0, col_start)
    ident = eye(statistic.shape, row_start, col_start)
    inverse_root = matmul(left, right, high) - (0.5390625 * scale) * statistic + 1.5380859375 * ident
    return (statistic, inverse_root)


def solution(mesh):
    return jax.shard_map(
        local,
        mesh=mesh,
        in_specs=(P("gx", "gy"), P("gx", "gy")),
        out_specs=(P("gx", "gy"), P("gx", "gy")),
        check_vma=False,
    )
```

time: 232 us -> 118 us (0.51)
  the two profiles are of different devices: /device:TPU:3 before, /device:TPU:0 now
where the time goes in v1:
time: 118 us
  blocking collectives  48.5 us (41%)
  waiting for transfers between devices  39.4 us (33%)
  between operations  14.8 us (13%)
  matrix products  14.3 us (12%)
    all_gather x1, waiting for transfers between devices, whole(): return lax.all_gather(rows, 'gx', axis=0, tiled=True)  39.4 us
    all_gather x1, blocking collectives, whole(): return lax.all_gather(rows, 'gx', axis=0, tiled=True)  32.7 us
    all_gather x2, blocking collectives, whole(): rows = lax.all_gather(block, 'gy', axis=1, tiled=True)  15.8 us
    dot_general x4, matrix products, matmul(): jnp.dot(leading, trailing, preferred_element_type=jnp.float32, precision=...  14.3 us
  transfers between devices with their start and end apart: 1, of which 1 were waited for; matrix products, arithmetic and copies ran while one was open for 0% of the time, Pallas kernels for 0%

profile of v1, /device:TPU:0, one launch (start us, length us, event | category | flops | bytes accessed | tf_op | source)
XLA Modules:
  0.0 118.1 jit_solution(12890260823301448606)
XLA Ops:
  7.2 0.0 all-gather.2.cloned.1.call-start
  7.2 10.3 %all_gather.12 = f32[128,1024]{1,0:T(8,128)} all-gather(f32[128,256]{1,0:T(8,128)} %param.3), channel_id=1, replica_groups=mesh['gx'=8,'gy'=4] {'gy'}, dimensions={1}, use_global_device_ids=true | all-gather | bytes 655360 | tf_op jit(solution)/shard_map/all_gather | solution.py:12
  17.5 0.0 all-gather.2.cloned.1.call-update
  17.6 5.4 %all_gather.14 = f32[128,128]{0,1:T(8,128)S(1)} all-gather(f32[128,32]{0,1:T(8,128)} %param.2), channel_id=1, replica_groups=mesh['gx'=8,'gy'=4] {'gy'}, dimensions={1}, use_global_device_ids=true | all-gather | bytes 81920 | tf_op jit(solution)/shard_map/all_gather | solution.py:12
  23.0 32.7 %all_gather.15 = f32[1024,128]{0,1:T(8,128)S(1)} all-gather(f32[128,128]{0,1:T(8,128)S(1)} %all_gather.14), channel_id=1, replica_groups=mesh['gx'=8,'gy'=4] {'gx'}, dimensions={0}, use_global_device_ids=true | all-gather | bytes 589824 | tf_op jit(solution)/shard_map/all_gather | solution.py:13
  55.8 39.4 %all-gather.2.cloned.1.call-done = f32[1024,1024]{1,0:T(8,128)} async-done(((f32[128,1024]{1,0:T(8,128)}), f32[1024,1024]{1,0:T(8,128)}) %all-gather.2.cloned.1.call-update) | async-done | bytes 4194320 | tf_op jit(solution)/shard_map/all_gather | solution.py:13
  95.1 7.3 %multiply_reduce_fusion = (f32[]{:T(128)}, f32[1024,1024]{1,0:T(8,128)}) fusion(f32[1024,128]{0,1:T(8,128)S(1)} %all_gather.15, f32[1024,1024]{1,0:T(8,128)} %all-gather.2.cloned.1.call-done), kind=kOutput, calls=%fused_computation | convolution fusion | flops 810549248 | bytes 8912900 | tf_op jit(solution)/shard_map/dot_general | solution.py:8
  103.1 0.0 copy-start
  103.1 4.0 %fusion.3 = f32[128,1024]{1,0:T(8,128)S(1)} fusion(f32[1024,1024]{1,0:T(8,128)} %get-tuple-element.3, s32[]{:T(128)S(6)} %select_n.11, s32[128]{0:T(128)S(1)} %iota_add_fusion.1, f32[]{:T(128)S(6)} %mul.84, f32[]{:T(128)S(6)} %mul.81), kind=kOutput, calls=%fused_computation.7 | convolution fusion | flops 806092800 | bytes 5769728 | tf_op jit(solution)/shard_map/dot_general | solution.py:8
  107.2 0.0 copy-done
  107.2 1.9 %fusion.1 = f32[1024,256]{1,0:T(8,128)S(1)} fusion(f32[1024,1024]{1,0:T(8,128)S(1)} %copy-done, s32[]{:T(128)S(6)} %select_n.13, s32[256]{0:T(256)S(1)} %iota_add_fusion, f32[]{:T(128)S(6)} %mul.84, f32[]{:T(128)S(6)} %mul.81), kind=kOutput, calls=%fused_computation.4 | convolution fusion | flops 1612185600 | bytes 7343104 | tf_op jit(solution)/shard_map/dot_general | solution.py:8
  109.1 1.0 dynamic_slice.9
  110.1 0.0 copy-start.1
  110.1 1.1 fusion.4
  111.2 0.0 copy-done.1
  (2 shorter events, 0.0 us)
Async XLA Ops:
  7.2 87.9 %all-gather.2.cloned.1.call-start = ((), (), s32[]{:S(2)}) async-start(), calls=%async_computation | async-start | bytes 4718592 | tf_op jit(solution)/shard_map/all_gather | solution.py:13
  103.1 4.0 %copy-start = (f32[1024,1024]{1,0:T(8,128)S(1)}, f32[1024,1024]{1,0:T(8,128)}, u32[]{:S(2)}) copy-start(f32[1024,1024]{1,0:T(8,128)} %get-tuple-element.3) | copy-start | bytes 12582916
  110.1 1.1 copy-start.1
Sparse Core Ops, SparseCore 0:
  17.7 77.3 all-gather.1

commit v2 on v1

v2 whole, which is shorter than its diff:
```python
import functools

import jax
import jax.numpy as jnp
from jax import lax
from jax.experimental import pallas as pl
from jax.experimental.pallas import tpu as pltpu
from jax.sharding import PartitionSpec as P

MESH = pl.DeviceIdType.MESH


def split(value):
    high = value.astype(jnp.bfloat16)
    return high, (value - high.astype(jnp.float32)).astype(jnp.bfloat16)


def dot3(left, right, dims):
    def one(a, b):
        return lax.dot_general(a, b, (dims, ((), ())), preferred_element_type=jnp.float32)

    return one(left[0], right[0]) + (one(left[0], right[1]) + one(left[1], right[0]))


def kernel(
    R, C, pay_ref, stat_ref, stat_out, root_out,
    buf, gt_hi, gt_lo, g_hi, g_lo, s_hi, s_lo, l_hi, l_lo, q_hi, q_lo, acc,
    send_sem, recv_sem, pair_sem, own_sem,
):
    height, width = stat_ref.shape
    payload = pay_ref.shape[0]
    part = payload // 2
    side = R * height
    X, Z, Y = 2, R // 2, C // 2
    row, col = lax.axis_index("gx"), lax.axis_index("gy")
    z, x, y, core = row // X, row % X, col // 2, col % 2
    x_other = 1 - x
    z_at = [z] + [lax.rem(z + k, Z) for k in range(1, Z)]
    y_at = [y] + [lax.rem(y + k, Y) for k in range(1, Y)]
    z_order = [k for pair in zip(range(1, Z), range(Z - 1, 0, -1)) for k in pair]
    z_order = list(dict.fromkeys(z_order))

    barrier = pltpu.get_barrier_semaphore()
    peers = [(z_at[k] * X + x, col) for k in range(1, Z)]
    peers += [(z * X + x_other, col)]
    peers += [(row, y_at[k] * 2 + core) for k in range(1, Y)]
    peers += [(row, y * 2 + (1 - core))]
    for peer in peers:
        pl.semaphore_signal(barrier, inc=1, device_id=peer, device_id_type=MESH)
    pl.semaphore_wait(barrier, len(peers))

    started = []

    def place(zz, xx, yy, cc, h):
        return buf.at[yy * 2 + cc, zz * X + xx, pl.ds(h * part, part), :]

    def slot(zz, xx, yy, h):
        return ((h * Z + zz) * X + xx) * Y + yy

    def send(src, zz, xx, yy, h, peer, arrive):
        copy = pltpu.make_async_remote_copy(
            src_ref=src,
            dst_ref=place(zz, xx, yy, core, h),
            send_sem=send_sem.at[len(started)],
            recv_sem=arrive.at[slot(zz, xx, yy, h)],
            device_id=peer,
            device_id_type=MESH,
        )
        copy.start()
        started.append(copy)

    def source(zz, xx, yy, h, own):
        return pay_ref.at[pl.ds(h * part, part), :] if own else place(zz, xx, yy, core, h)

    def to_x(zz, yy, h, own=False):
        send(source(zz, x, yy, h, own), zz, x, yy, h, (z * X + x_other, col), recv_sem)

    def to_y(zz, xx, h, own=False):
        for k in range(1, Y):
            send(source(zz, xx, y, h, own), zz, xx, y, h, (row, y_at[k] * 2 + core), recv_sem)

    def to_pair(zz, xx, yy, h, own=False):
        send(source(zz, xx, yy, h, own), zz, xx, yy, h, (row, y * 2 + (1 - core)), pair_sem)

    def arrived(zz, xx, yy, cc, h, sem):
        here = place(zz, xx, yy, cc, h)
        pltpu.make_async_copy(here, here, sem.at[slot(zz, xx, yy, h)]).wait()

    own_copy = pltpu.make_async_copy(pay_ref, buf.at[col, row], own_sem)
    own_copy.start()
    to_x(z, y, 0, True)
    to_y(z, x, 1, True)
    for k in z_order:
        for h in range(2):
            send(source(z, x, y, h, True), z, x, y, h, (z_at[k] * X + x, col), recv_sem)
    to_x(z, y, 1, True)
    to_y(z, x, 0, True)
    for h in range(2):
        to_pair(z, x, y, h, True)

    def second_leg(zz):
        arrived(zz, x_other, y, core, 0, recv_sem)
        to_y(zz, x_other, 0)
        to_pair(zz, x_other, y, 0)
        for k in range(1, Y):
            arrived(zz, x, y_at[k], core, 1, recv_sem)
            to_x(zz, y_at[k], 1)
            to_pair(zz, x, y_at[k], 1)

    second_leg(z)
    for k in z_order:
        zz = z_at[k]
        for h in range(2):
            arrived(zz, x, y, core, h, recv_sem)
        to_x(zz, y, 0)
        to_y(zz, x, 1)
        to_x(zz, y, 1)
        to_y(zz, x, 0)
        for h in range(2):
            to_pair(zz, x, y, h)
    for k in z_order:
        second_leg(z_at[k])
    for k in [0] + z_order:
        zz = z_at[k]
        arrived(zz, x_other, y, core, 1, recv_sem)
        to_pair(zz, x_other, y, 1)
        for k in range(1, Y):
            arrived(zz, x, y_at[k], core, 0, recv_sem)
            to_pair(zz, x, y_at[k], 0)
    for k in [0] + z_order:
        zz = z_at[k]
        for k in range(1, Y):
            for h in range(2):
                arrived(zz, x_other, y_at[k], core, h, recv_sem)
                to_pair(zz, x_other, y_at[k], h)
    for k in [0] + z_order:
        for xx in range(X):
            for yy in range(Y):
                for h in range(2):
                    arrived(z_at[k], xx, yy, 1 - core, h, pair_sem)
    own_copy.wait()

    pieces = width // height
    step = payload - height
    for i in range(R):
        for j in range(C):
            for l in range(pieces):
                at = (j * pieces + l) * step
                value = buf[j, i, height:, l * height:(l + 1) * height]
                high, low = split(value)
                gt_hi[at:at + step, i * height:(i + 1) * height] = high
                gt_lo[at:at + step, i * height:(i + 1) * height] = low
    depth = gt_hi.shape[0]

    def turn(i, carry):
        here = pl.ds(pl.multiple_of(i * height, height), height)
        g_hi[here, :] = gt_hi[:, here].T
        g_lo[here, :] = gt_lo[:, here].T
        return carry

    lax.fori_loop(0, R, turn, 0)

    def outer(here, there):
        return dot3(
            (g_hi[here, :], g_lo[here, :]), (gt_hi[:, there], gt_lo[:, there]), ((1,), (0,))
        ) * (1.0 / depth)

    acc[...] = jnp.zeros_like(acc)

    def assemble(i, carry):
        here = pl.ds(pl.multiple_of(i * height, height), height)
        for j in range(C):
            there = slice(j * width, (j + 1) * width)
            value = 0.9 * buf[j, i, :height, :] + outer(here, there)
            acc[...] += value * value
            high, low = split(value)
            s_hi[here, there] = high
            s_lo[here, there] = low
        return carry

    lax.fori_loop(0, R, assemble, 0)
    my_rows = pl.ds(pl.multiple_of(row * height, height), height)
    my_cols = pl.ds(pl.multiple_of(col * width, width), width)
    statistic = 0.9 * stat_ref[...] + outer(my_rows, my_cols)
    stat_out[...] = statistic
    total = jnp.sum(jnp.sum(acc[...], axis=0, keepdims=True), axis=1, keepdims=True)
    scale = 0.5 / jnp.sqrt(total / side)

    for store, kept in ((l_hi, s_hi), (l_lo, s_lo)):
        store[:height, :] = kept[my_rows, :]
        store[height:, :] = kept[my_cols, :]

    left_rows = height + width
    line = lax.broadcasted_iota(jnp.int32, (left_rows, width), 0)
    line = jnp.where(line < height, row * height + line, col * width + line - height)
    across = lax.broadcasted_iota(jnp.int32, (left_rows, width), 1)

    def square(j, carry):
        there = pl.ds(pl.multiple_of(j * width, width), width)
        value = dot3((l_hi[...], l_lo[...]), (s_hi[:, there], s_lo[:, there]), ((1,), (0,)))
        panel = l_hi[:, there].astype(jnp.float32) + l_lo[:, there].astype(jnp.float32)
        ident = jnp.where(line == across + j * width, 0.84375, 0.0)
        quad = (0.25 * scale * scale) * value - (1.125 * scale) * panel + ident
        high, low = split(quad)
        q_hi[:, there] = high
        q_lo[:, there] = low
        return carry

    lax.fori_loop(0, C, square, 0)
    root = dot3(
        (q_hi[:height, :], q_lo[:height, :]), (q_hi[height:, :], q_lo[height:, :]), ((1,), (1,))
    )
    rows = row * height + lax.broadcasted_iota(jnp.int32, (height, width), 0)
    cols = col * width + lax.broadcasted_iota(jnp.int32, (height, width), 1)
    root_out[...] = (
        root - (0.5390625 * scale) * statistic + jnp.where(rows == cols, 1.5380859375, 0.0)
    )
    for copy in started:
        copy.wait_send()


def local(R, C, gradient, stat_old):
    height, width = stat_old.shape
    pieces = width // height
    lines = gradient.shape[1] // pieces
    turned = gradient.T
    extra = jnp.concatenate([turned[l * lines:(l + 1) * lines] for l in range(pieces)], axis=1)
    pay = jnp.concatenate([stat_old, extra], axis=0)
    payload = pay.shape[0]
    side, depth = R * height, C * gradient.shape[1]
    Z, X, Y = R // 2, 2, C // 2
    chips = Z * X * Y
    sends = 2 * (Z - 1) + 2 * Z + Z * (Y - 1) + (3 * Z) * (Y - 1) + 2 * chips
    half = jnp.bfloat16
    vmem = pl.BlockSpec(memory_space=pltpu.VMEM)
    return pl.pallas_call(
        functools.partial(kernel, R, C),
        out_shape=(jax.ShapeDtypeStruct(stat_old.shape, jnp.float32),) * 2,
        in_specs=[vmem] * 2,
        out_specs=(vmem,) * 2,
        scratch_shapes=[
            pltpu.VMEM((C, R, payload, width), jnp.float32),
            pltpu.VMEM((depth, side), half),
            pltpu.VMEM((depth, side), half),
            pltpu.VMEM((side, depth), half),
            pltpu.VMEM((side, depth), half),
            pltpu.VMEM((side, side), half),
            pltpu.VMEM((side, side), half),
            pltpu.VMEM((height + width, side), half),
            pltpu.VMEM((height + width, side), half),
            pltpu.VMEM((height + width, side), half),
            pltpu.VMEM((height + width, side), half),
            pltpu.VMEM((height, width), jnp.float32),
            pltpu.SemaphoreType.DMA((sends,)),
            pltpu.SemaphoreType.DMA((2 * chips,)),
            pltpu.SemaphoreType.DMA((2 * chips,)),
            pltpu.SemaphoreType.DMA,
        ],
        compiler_params=pltpu.CompilerParams(collective_id=0, has_side_effects=True),
    )(pay, stat_old)


def solution(mesh):
    return jax.shard_map(
        functools.partial(local, mesh.shape["gx"], mesh.shape["gy"]),
        mesh=mesh,
        in_specs=(P("gx", "gy"), P("gx", "gy")),
        out_specs=(P("gx", "gy"), P("gx", "gy")),
        check_vma=False,
    )
```

time: 118 us -> 45.7 us (0.39)
  the two profiles are of different devices: /device:TPU:0 before, /device:TPU:1 now
where the time goes in v2:
time: 45.7 us; the launch traced here: 45.5 us
  Pallas kernels  40.3 us (88%)
  local copies, waits for them, and re-layouts  2.98 us (7%)
  other arithmetic  1.56 us (3%)
  between operations  0.65 us (1%)
    pallas_call x1, Pallas kernels, local(): pl.pallas_call(functools.partial(kernel, R, C), out_shape=(jax.ShapeDtype...  40.3 us
    unnamed x4, local copies, waits for them, and re-layouts  2.26 us
    concatenate x1, other arithmetic, local(): pay = jnp.concatenate([stat_old, extra], axis=0)  1.56 us

profile of v2, /device:TPU:1, one launch (start us, length us, event | category | flops | bytes accessed | tf_op | source)
XLA Modules:
  0.0 45.5 jit_solution(4114139711472946317)
XLA Ops:
  0.6 0.7 %fusion = (f32[16,128]{1,0:T(8,128)S(1)}, f32[16,128]{1,0:T(8,128)S(1)}) fusion(f32[32,128]{1,0:T(8,128)} %bitcast.1), kind=kLoop, calls=%fused_computation.1 | loop fusion | bytes 32768 | tf_op jit(solution)/shard_map/slice | solution.py:227
  1.3 1.6 %maximum_maximum_fusion.pay_ref = f32[144,256]{1,0:T(8,128)} fusion(f32[16,128]{1,0:T(8,128)S(1)} %get-tuple-element.3, f32[16,128]{1,0:T(8,128)S(1)} %get-tuple-element.2, f32[128,256]{1,0:T(8,128)} %stat_ref.1), kind=kLoop, calls=%fused_computation | loop fusion | flops 73728 | bytes 294912 | tf_op jit(solution)/shard_map/concatenate | solution.py:228
  2.9 40.3 %shard_map.41 = (f32[128,256]{1,0:T(8,128)}, f32[128,256]{1,0:T(8,128)}) custom-call(f32[144,256]{1,0:T(8,128)} %maximum_maximum_fusion.pay_ref, f32[128,256]{1,0:T(8,128)} %stat_ref.1), custom_call_target="tpu_custom_call" | custom-call | tf_op jit(solution)/shard_map/pallas_call | solution.py:236
  43.2 0.0 copy-start
  43.2 1.6 %copy.6 = f32[128,256]{1,0:T(8,128)} copy(f32[128,256]{1,0:T(8,128)} %get-tuple-element.6) | data formatting | bytes 262144
  44.8 0.0 copy-done
  44.8 0.7 %copy.7 = f32[128,256]{1,0:T(8,128)} copy(f32[128,256]{1,0:T(8,128)S(1)} %copy-done) | data formatting | bytes 262144
Async XLA Ops:
  43.2 1.6 %copy-start = (f32[128,256]{1,0:T(8,128)S(1)}, f32[128,256]{1,0:T(8,128)}, u32[]{:S(2)}) copy-start(f32[128,256]{1,0:T(8,128)} %get-tuple-element.7) | copy-start | bytes 393220

commit v3 on v2

--- a/solution.py
+++ b/solution.py
@@ -22,15 +22,25 @@
     return one(left[0], right[0]) + (one(left[0], right[1]) + one(left[1], right[0]))
 
 
+def mirror(R, C, height, width):
+    return width == 2 * height and R == 2 * C
+
+
+def chosen(i, j):
+    odd = i % 2
+    return jnp.where(i >= 2 * j, odd, 1 - odd)
+
+
 def kernel(
     R, C, pay_ref, stat_ref, stat_out, root_out,
-    buf, gt_hi, gt_lo, g_hi, g_lo, s_hi, s_lo, l_hi, l_lo, q_hi, q_lo, acc,
-    send_sem, recv_sem, pair_sem, own_sem,
+    buf, spare, gt, g, s_hi, s_lo, l_hi, l_lo, q_hi, q_lo, acc,
+    send_sem, recv_sem, pair_sem, own_sem, spare_send, spare_recv, spare_pair,
 ):
     height, width = stat_ref.shape
     payload = pay_ref.shape[0]
     part = payload // 2
     side = R * height
+    mirrored = mirror(R, C, height, width)
     X, Z, Y = 2, R // 2, C // 2
     row, col = lax.axis_index("gx"), lax.axis_index("gy")
     z, x, y, core = row // X, row % X, col // 2, col % 2
@@ -57,42 +67,78 @@
     def slot(zz, xx, yy, h):
         return ((h * Z + zz) * X + xx) * Y + yy
 
-    def send(src, zz, xx, yy, h, peer, arrive):
+    def both(zz, xx, yy, cc):
+        return jnp.logical_and(xx == 0, yy * 2 + cc == zz)
+
+    def spare_place(zz, h):
+        return spare.at[zz, pl.ds(h * (height // 2), height // 2), :]
+
+    def send(src, zz, xx, yy, h, peer, pair=False):
         copy = pltpu.make_async_remote_copy(
             src_ref=src,
             dst_ref=place(zz, xx, yy, core, h),
             send_sem=send_sem.at[len(started)],
-            recv_sem=arrive.at[slot(zz, xx, yy, h)],
+            recv_sem=(pair_sem if pair else recv_sem).at[slot(zz, xx, yy, h)],
             device_id=peer,
             device_id_type=MESH,
         )
         copy.start()
-        started.append(copy)
+        more = None
+        if mirrored:
+            own = src is not None and src_is_own[0]
+            start = (
+                stat_ref.at[pl.ds(h * (height // 2), height // 2), pl.ds(height, height)]
+                if own
+                else spare_place(zz, h)
+            )
+            more = pltpu.make_async_remote_copy(
+                src_ref=start,
+                dst_ref=spare_place(zz, h),
+                send_sem=spare_send.at[len(started)],
+                recv_sem=(spare_pair if pair else spare_recv).at[h * Z + zz],
+                device_id=peer,
+                device_id_type=MESH,
+            )
+            pl.when(both(zz, xx, yy, core))(more.start)
+        started.append((copy, more, both(zz, xx, yy, core)))
+
+    src_is_own = [False]
 
     def source(zz, xx, yy, h, own):
+        src_is_own[0] = own
         return pay_ref.at[pl.ds(h * part, part), :] if own else place(zz, xx, yy, core, h)
 
     def to_x(zz, yy, h, own=False):
-        send(source(zz, x, yy, h, own), zz, x, yy, h, (z * X + x_other, col), recv_sem)
+        send(source(zz, x, yy, h, own), zz, x, yy, h, (z * X + x_other, col))
 
     def to_y(zz, xx, h, own=False):
         for k in range(1, Y):
-            send(source(zz, xx, y, h, own), zz, xx, y, h, (row, y_at[k] * 2 + core), recv_sem)
+            send(source(zz, xx, y, h, own), zz, xx, y, h, (row, y_at[k] * 2 + core))
 
     def to_pair(zz, xx, yy, h, own=False):
-        send(source(zz, xx, yy, h, own), zz, xx, yy, h, (row, y * 2 + (1 - core)), pair_sem)
+        send(source(zz, xx, yy, h, own), zz, xx, yy, h, (row, y * 2 + (1 - core)), True)
 
     def arrived(zz, xx, yy, cc, h, sem):
         here = place(zz, xx, yy, cc, h)
         pltpu.make_async_copy(here, here, sem.at[slot(zz, xx, yy, h)]).wait()
-
-    own_copy = pltpu.make_async_copy(pay_ref, buf.at[col, row], own_sem)
+        if mirrored:
+            there = spare_place(zz, h)
+            sems = spare_pair if sem is pair_sem else spare_recv
+            more = pltpu.make_async_copy(there, there, sems.at[h * Z + zz])
+            pl.when(both(zz, xx, yy, cc))(more.wait)
+
+    own_copy = pltpu.make_async_copy(pay_ref, buf.at[col, row], own_sem.at[0])
     own_copy.start()
+    if mirrored:
+        own_more = pltpu.make_async_copy(
+            stat_ref.at[:, pl.ds(height, height)], spare.at[z], own_sem.at[1]
+        )
+        pl.when(both(z, x, y, core))(own_more.start)
     to_x(z, y, 0, True)
     to_y(z, x, 1, True)
     for k in z_order:
         for h in range(2):
-            send(source(z, x, y, h, True), z, x, y, h, (z_at[k] * X + x, col), recv_sem)
+            send(source(z, x, y, h, True), z, x, y, h, (z_at[k] * X + x, col))
     to_x(z, y, 1, True)
     to_y(z, x, 0, True)
     for h in range(2):
@@ -139,46 +185,60 @@
                 for h in range(2):
                     arrived(z_at[k], xx, yy, 1 - core, h, pair_sem)
     own_copy.wait()
-
-    pieces = width // height
+    if mirrored:
+        pl.when(both(z, x, y, core))(own_more.wait)
+
     step = payload - height
+    depth = C * step
     for i in range(R):
         for j in range(C):
-            for l in range(pieces):
-                at = (j * pieces + l) * step
-                value = buf[j, i, height:, l * height:(l + 1) * height]
-                high, low = split(value)
-                gt_hi[at:at + step, i * height:(i + 1) * height] = high
-                gt_lo[at:at + step, i * height:(i + 1) * height] = low
-    depth = gt_hi.shape[0]
+            at = j * step
+            here = slice(i * height, (i + 1) * height)
+            high, low = split(buf[j, i, height:, :])
+            gt[at:at + step, here] = high
+            gt[depth + at:depth + at + step, here] = low
+            gt[2 * depth + at:2 * depth + at + step, here] = high
 
     def turn(i, carry):
         here = pl.ds(pl.multiple_of(i * height, height), height)
-        g_hi[here, :] = gt_hi[:, here].T
-        g_lo[here, :] = gt_lo[:, here].T
+        high = gt[:depth, here].T
+        g[here, :depth] = high
+        g[here, depth:2 * depth] = high
+        g[here, 2 * depth:] = gt[depth:2 * depth, here].T
         return carry
 
     lax.fori_loop(0, R, turn, 0)
 
     def outer(here, there):
-        return dot3(
-            (g_hi[here, :], g_lo[here, :]), (gt_hi[:, there], gt_lo[:, there]), ((1,), (0,))
-        ) * (1.0 / depth)
+        return jnp.dot(g[here, :], gt[:, there], preferred_element_type=jnp.float32) * (1.0 / depth)
 
     acc[...] = jnp.zeros_like(acc)
 
+    def put(value, a, b):
+        here = pl.ds(pl.multiple_of(a * height, height), height)
+        there = pl.ds(pl.multiple_of(b * height, height), height)
+        value = 0.9 * value + outer(here, there)
+        times = jnp.where(a == b, 1.0, 2.0) if mirrored else 1.0
+        acc[...] += times * (value * value)
+        high, low = split(value)
+        s_hi[here, there] = high
+        s_lo[here, there] = low
+        if mirrored:
+            s_hi[there, here] = high.T
+            s_lo[there, here] = low.T
+
     def assemble(i, carry):
-        here = pl.ds(pl.multiple_of(i * height, height), height)
         for j in range(C):
-            there = slice(j * width, (j + 1) * width)
-            value = 0.9 * buf[j, i, :height, :] + outer(here, there)
-            acc[...] += value * value
-            high, low = split(value)
-            s_hi[here, there] = high
-            s_lo[here, there] = low
+            put(buf[j, i, :height, :], i, 2 * j + chosen(i, j) if mirrored else j)
         return carry
 
     lax.fori_loop(0, R, assemble, 0)
+    if mirrored:
+        def assemble_spare(n, carry):
+            put(spare[n], 2 * n, 2 * n + 1)
+            return carry
+
+        lax.fori_loop(0, Z, assemble_spare, 0)
     my_rows = pl.ds(pl.multiple_of(row * height, height), height)
     my_cols = pl.ds(pl.multiple_of(col * width, width), width)
     statistic = 0.9 * stat_ref[...] + outer(my_rows, my_cols)
@@ -215,17 +275,21 @@
     root_out[...] = (
         root - (0.5390625 * scale) * statistic + jnp.where(rows == cols, 1.5380859375, 0.0)
     )
-    for copy in started:
+    for copy, more, wanted in started:
         copy.wait_send()
+        if mirrored:
+            pl.when(wanted)(more.wait_send)
 
 
 def local(R, C, gradient, stat_old):
     height, width = stat_old.shape
-    pieces = width // height
-    lines = gradient.shape[1] // pieces
+    mirrored = mirror(R, C, height, width)
     turned = gradient.T
-    extra = jnp.concatenate([turned[l * lines:(l + 1) * lines] for l in range(pieces)], axis=1)
-    pay = jnp.concatenate([stat_old, extra], axis=0)
+    main = stat_old
+    if mirrored:
+        pick = chosen(lax.axis_index("gx"), lax.axis_index("gy"))
+        main = jnp.where(pick == 0, stat_old[:, :height], stat_old[:, height:])
+    pay = jnp.concatenate([main, turned], axis=0)
     payload = pay.shape[0]
     side, depth = R * height, C * gradient.shape[1]
     Z, X, Y = R // 2, 2, C // 2
@@ -239,22 +303,24 @@
         in_specs=[vmem] * 2,
         out_specs=(vmem,) * 2,
         scratch_shapes=[
-            pltpu.VMEM((C, R, payload, width), jnp.float32),
-            pltpu.VMEM((depth, side), half),
-            pltpu.VMEM((depth, side), half),
-            pltpu.VMEM((side, depth), half),
-            pltpu.VMEM((side, depth), half),
+            pltpu.VMEM((C, R, payload, height), jnp.float32),
+            pltpu.VMEM((Z, height, height), jnp.float32),
+            pltpu.VMEM((3 * depth, side), half),
+            pltpu.VMEM((side, 3 * depth), half),
             pltpu.VMEM((side, side), half),
             pltpu.VMEM((side, side), half),
             pltpu.VMEM((height + width, side), half),
             pltpu.VMEM((height + width, side), half),
             pltpu.VMEM((height + width, side), half),
             pltpu.VMEM((height + width, side), half),
-            pltpu.VMEM((height, width), jnp.float32),
+            pltpu.VMEM((height, height), jnp.float32),
             pltpu.SemaphoreType.DMA((sends,)),
             pltpu.SemaphoreType.DMA((2 * chips,)),
             pltpu.SemaphoreType.DMA((2 * chips,)),
-            pltpu.SemaphoreType.DMA,
+            pltpu.SemaphoreType.DMA((2,)),
+            pltpu.SemaphoreType.DMA((sends if mirrored else 1,)),
+            pltpu.SemaphoreType.DMA((2 * Z,)),
+            pltpu.SemaphoreType.DMA((2 * Z,)),
         ],
         compiler_params=pltpu.CompilerParams(collective_id=0, has_side_effects=True),
     )(pay, stat_old)

time: 45.7 us -> 40.4 us (0.88)
  the two profiles are of different devices: /device:TPU:1 before, /device:TPU:3 now
where the time goes in v3:
time: 40.4 us; the launch traced here: 40.2 us
  Pallas kernels  35.7 us (88%)
  local copies, waits for them, and re-layouts  2.27 us (6%)
  other arithmetic  1.53 us (4%)
  between operations  0.68 us (2%)
    pallas_call x1, Pallas kernels, local(): pl.pallas_call(functools.partial(kernel, R, C), out_shape=(jax.ShapeDtype...  35.7 us
    unnamed x6, local copies, waits for them, and re-layouts  2.27 us
    select_n x1, other arithmetic, local(): main = jnp.where(pick == 0, stat_old[:, :height], stat_old[:, height:])  0.89 us

profile of v3, /device:TPU:3, one launch (start us, length us, event | category | flops | bytes accessed | tf_op | source)
XLA Modules:
  0.0 40.2 jit_solution(14859647249927366576)
XLA Ops:
  0.6 0.0 copy-start.1
  0.7 0.9 %slice_select_fusion = f32[128,128]{1,0:T(8,128)S(1)} fusion(f32[128,256]{1,0:T(8,128)} %stat_ref.1, pred[]{:T(512)S(6)} %eq.5), kind=kLoop, calls=%fused_computation.1 | loop fusion | flops 16384 | bytes 196609 | tf_op jit(solution)/shard_map/jit(_where)/select_n | solution.py:291
  1.5 0.0 copy-done.1
  1.6 0.6 %pad_maximum_fusion.pay_ref = f32[160,128]{1,0:T(8,128)} fusion(f32[32,128]{1,0:T(8,128)S(1)} %bitcast.1, f32[128,128]{1,0:T(8,128)S(1)} %slice_select_fusion), kind=kLoop, calls=%fused_computation | loop fusion | flops 20480 | bytes 163840 | tf_op jit(solution)/shard_map/concatenate | solution.py:292
  2.2 35.7 %shard_map.41 = (f32[128,256]{1,0:T(8,128)}, f32[128,256]{1,0:T(8,128)}) custom-call(f32[160,128]{1,0:T(8,128)} %pad_maximum_fusion.pay_ref, f32[128,256]{1,0:T(8,128)} %stat_ref.1), custom_call_target="tpu_custom_call" | custom-call | tf_op jit(solution)/shard_map/pallas_call | solution.py:300
  37.9 0.0 copy-start
  37.9 1.6 %copy.6 = f32[128,256]{1,0:T(8,128)} copy(f32[128,256]{1,0:T(8,128)} %get-tuple-element.4) | data formatting | bytes 262144
  39.5 0.0 copy-done
  39.5 0.7 %copy.7 = f32[128,256]{1,0:T(8,128)} copy(f32[128,256]{1,0:T(8,128)S(1)} %copy-done) | data formatting | bytes 262144
Async XLA Ops:
  0.6 0.9 %copy-start.1 = (f32[128,32]{0,1:T(8,128)S(1)}, f32[128,32]{0,1:T(8,128)}, u32[]{:S(2)}) copy-start(f32[128,32]{0,1:T(8,128)} %param.2) | copy-start | bytes 49156
  37.9 1.6 %copy-start = (f32[128,256]{1,0:T(8,128)S(1)}, f32[128,256]{1,0:T(8,128)}, u32[]{:S(2)}) copy-start(f32[128,256]{1,0:T(8,128)} %get-tuple-element.5) | copy-start | bytes 393220

commit v4 on v3

--- a/solution.py
+++ b/solution.py
@@ -8,6 +8,7 @@
 from jax.sharding import PartitionSpec as P
 
 MESH = pl.DeviceIdType.MESH
+BOTH = 2
 
 
 def split(value):
@@ -38,7 +39,6 @@
 ):
     height, width = stat_ref.shape
     payload = pay_ref.shape[0]
-    part = payload // 2
     side = R * height
     mirrored = mirror(R, C, height, width)
     X, Z, Y = 2, R // 2, C // 2
@@ -61,17 +61,20 @@
 
     started = []
 
+    def lines(h, total):
+        return pl.ds(0, total) if h == BOTH else pl.ds(h * (total // 2), total // 2)
+
     def place(zz, xx, yy, cc, h):
-        return buf.at[yy * 2 + cc, zz * X + xx, pl.ds(h * part, part), :]
+        return buf.at[yy * 2 + cc, zz * X + xx, lines(h, payload), :]
 
     def slot(zz, xx, yy, h):
-        return ((h * Z + zz) * X + xx) * Y + yy
+        return (((h % BOTH) * Z + zz) * X + xx) * Y + yy
 
     def both(zz, xx, yy, cc):
         return jnp.logical_and(xx == 0, yy * 2 + cc == zz)
 
     def spare_place(zz, h):
-        return spare.at[zz, pl.ds(h * (height // 2), height // 2), :]
+        return spare.at[zz, lines(h, height), :]
 
     def send(src, zz, xx, yy, h, peer, pair=False):
         copy = pltpu.make_async_remote_copy(
@@ -85,9 +88,9 @@
         copy.start()
         more = None
         if mirrored:
-            own = src is not None and src_is_own[0]
+            own = src_is_own[0]
             start = (
-                stat_ref.at[pl.ds(h * (height // 2), height // 2), pl.ds(height, height)]
+                stat_ref.at[lines(h, height), pl.ds(height, height)]
                 if own
                 else spare_place(zz, h)
             )
@@ -95,7 +98,7 @@
                 src_ref=start,
                 dst_ref=spare_place(zz, h),
                 send_sem=spare_send.at[len(started)],
-                recv_sem=(spare_pair if pair else spare_recv).at[h * Z + zz],
+                recv_sem=(spare_pair if pair else spare_recv).at[(h % BOTH) * Z + zz],
                 device_id=peer,
                 device_id_type=MESH,
             )
@@ -106,7 +109,7 @@
 
     def source(zz, xx, yy, h, own):
         src_is_own[0] = own
-        return pay_ref.at[pl.ds(h * part, part), :] if own else place(zz, xx, yy, core, h)
+        return pay_ref.at[lines(h, payload), :] if own else place(zz, xx, yy, core, h)
 
     def to_x(zz, yy, h, own=False):
         send(source(zz, x, yy, h, own), zz, x, yy, h, (z * X + x_other, col))
@@ -124,7 +127,7 @@
         if mirrored:
             there = spare_place(zz, h)
             sems = spare_pair if sem is pair_sem else spare_recv
-            more = pltpu.make_async_copy(there, there, sems.at[h * Z + zz])
+            more = pltpu.make_async_copy(there, there, sems.at[(h % BOTH) * Z + zz])
             pl.when(both(zz, xx, yy, cc))(more.wait)
 
     own_copy = pltpu.make_async_copy(pay_ref, buf.at[col, row], own_sem.at[0])
@@ -134,56 +137,40 @@
             stat_ref.at[:, pl.ds(height, height)], spare.at[z], own_sem.at[1]
         )
         pl.when(both(z, x, y, core))(own_more.start)
-    to_x(z, y, 0, True)
-    to_y(z, x, 1, True)
+    to_x(z, y, BOTH, True)
+    to_y(z, x, BOTH, True)
     for k in z_order:
-        for h in range(2):
-            send(source(z, x, y, h, True), z, x, y, h, (z_at[k] * X + x, col))
-    to_x(z, y, 1, True)
-    to_y(z, x, 0, True)
-    for h in range(2):
-        to_pair(z, x, y, h, True)
+        send(source(z, x, y, BOTH, True), z, x, y, BOTH, (z_at[k] * X + x, col))
+    to_pair(z, x, y, BOTH, True)
 
     def second_leg(zz):
-        arrived(zz, x_other, y, core, 0, recv_sem)
+        arrived(zz, x_other, y, core, BOTH, recv_sem)
         to_y(zz, x_other, 0)
-        to_pair(zz, x_other, y, 0)
         for k in range(1, Y):
-            arrived(zz, x, y_at[k], core, 1, recv_sem)
+            arrived(zz, x, y_at[k], core, BOTH, recv_sem)
             to_x(zz, y_at[k], 1)
-            to_pair(zz, x, y_at[k], 1)
+            to_pair(zz, x, y_at[k], BOTH)
+        to_pair(zz, x_other, y, BOTH)
 
     second_leg(z)
     for k in z_order:
         zz = z_at[k]
-        for h in range(2):
-            arrived(zz, x, y, core, h, recv_sem)
-        to_x(zz, y, 0)
-        to_y(zz, x, 1)
-        to_x(zz, y, 1)
-        to_y(zz, x, 0)
-        for h in range(2):
-            to_pair(zz, x, y, h)
+        arrived(zz, x, y, core, BOTH, recv_sem)
+        to_x(zz, y, BOTH)
+        to_y(zz, x, BOTH)
+        to_pair(zz, x, y, BOTH)
     for k in z_order:
         second_leg(z_at[k])
     for k in [0] + z_order:
         zz = z_at[k]
-        arrived(zz, x_other, y, core, 1, recv_sem)
-        to_pair(zz, x_other, y, 1)
-        for k in range(1, Y):
-            arrived(zz, x, y_at[k], core, 0, recv_sem)
-            to_pair(zz, x, y_at[k], 0)
-    for k in [0] + z_order:
-        zz = z_at[k]
-        for k in range(1, Y):
+        for n in range(1, Y):
             for h in range(2):
-                arrived(zz, x_other, y_at[k], core, h, recv_sem)
-                to_pair(zz, x_other, y_at[k], h)
+                arrived(zz, x_other, y_at[n], core, h, recv_sem)
+            to_pair(zz, x_other, y_at[n], BOTH)
     for k in [0] + z_order:
         for xx in range(X):
             for yy in range(Y):
-                for h in range(2):
-                    arrived(z_at[k], xx, yy, 1 - core, h, pair_sem)
+                arrived(z_at[k], xx, yy, 1 - core, BOTH, pair_sem)
     own_copy.wait()
     if mirrored:
         pl.when(both(z, x, y, core))(own_more.wait)
@@ -257,7 +244,9 @@
 
     def square(j, carry):
         there = pl.ds(pl.multiple_of(j * width, width), width)
-        value = dot3((l_hi[...], l_lo[...]), (s_hi[:, there], s_lo[:, there]), ((1,), (0,)))
+        rounded = s_hi[:, there]
+        value = jnp.dot(l_hi[...], rounded, preferred_element_type=jnp.float32)
+        value += jnp.dot(l_lo[...], rounded, preferred_element_type=jnp.float32)
         panel = l_hi[:, there].astype(jnp.float32) + l_lo[:, there].astype(jnp.float32)
         ident = jnp.where(line == across + j * width, 0.84375, 0.0)
         quad = (0.25 * scale * scale) * value - (1.125 * scale) * panel + ident
@@ -294,7 +283,7 @@
     side, depth = R * height, C * gradient.shape[1]
     Z, X, Y = R // 2, 2, C // 2
     chips = Z * X * Y
-    sends = 2 * (Z - 1) + 2 * Z + Z * (Y - 1) + (3 * Z) * (Y - 1) + 2 * chips
+    sends = (Z - 1) + Z + 3 * Z * (Y - 1) + chips
     half = jnp.bfloat16
     vmem = pl.BlockSpec(memory_space=pltpu.VMEM)
     return pl.pallas_call(

time: 40.4 us -> 39.8 us (0.985)
  Pallas kernels: 35.7 us -> 35.2 us
    pallas_call x1, Pallas kernels: 35.7 us -> 35.2 us  [local(): pl.pallas_call(functools.partial(kernel, R, C), out_shape=(jax.ShapeDtype...]
where the time goes in v4:
time: 39.8 us; the launch traced here: 39.6 us
  Pallas kernels  35.2 us (88%)
  local copies, waits for them, and re-layouts  2.27 us (6%)
  other arithmetic  1.53 us (4%)
  between operations  0.68 us (2%)
    pallas_call x1, Pallas kernels, local(): pl.pallas_call(functools.partial(kernel, R, C), out_shape=(jax.ShapeDtype...  35.2 us
    unnamed x6, local copies, waits for them, and re-layouts  2.27 us
    select_n x1, other arithmetic, local(): main = jnp.where(pick == 0, stat_old[:, :height], stat_old[:, height:])  0.89 us

profile of v4, /device:TPU:3, one launch (start us, length us, event | category | flops | bytes accessed | tf_op | source)
XLA Modules:
  0.0 39.6 jit_solution(17713786624962570745)
XLA Ops:
  0.6 0.0 copy-start.1
  0.7 0.9 %slice_select_fusion = f32[128,128]{1,0:T(8,128)S(1)} fusion(f32[128,256]{1,0:T(8,128)} %stat_ref.1, pred[]{:T(512)S(6)} %eq.5), kind=kLoop, calls=%fused_computation.1 | loop fusion | flops 16384 | bytes 196609 | tf_op jit(solution)/shard_map/jit(_where)/select_n | solution.py:280
  1.5 0.0 copy-done.1
  1.6 0.6 %pad_maximum_fusion.pay_ref = f32[160,128]{1,0:T(8,128)} fusion(f32[32,128]{1,0:T(8,128)S(1)} %bitcast.1, f32[128,128]{1,0:T(8,128)S(1)} %slice_select_fusion), kind=kLoop, calls=%fused_computation | loop fusion | flops 20480 | bytes 163840 | tf_op jit(solution)/shard_map/concatenate | solution.py:281
  2.2 35.2 %shard_map.41 = (f32[128,256]{1,0:T(8,128)}, f32[128,256]{1,0:T(8,128)}) custom-call(f32[160,128]{1,0:T(8,128)} %pad_maximum_fusion.pay_ref, f32[128,256]{1,0:T(8,128)} %stat_ref.1), custom_call_target="tpu_custom_call" | custom-call | tf_op jit(solution)/shard_map/pallas_call | solution.py:289
  37.4 0.0 copy-start
  37.4 1.6 %copy.6 = f32[128,256]{1,0:T(8,128)} copy(f32[128,256]{1,0:T(8,128)} %get-tuple-element.4) | data formatting | bytes 262144
  39.0 0.0 copy-done
  39.0 0.7 %copy.7 = f32[128,256]{1,0:T(8,128)} copy(f32[128,256]{1,0:T(8,128)S(1)} %copy-done) | data formatting | bytes 262144
Async XLA Ops:
  0.6 0.9 %copy-start.1 = (f32[128,32]{0,1:T(8,128)S(1)}, f32[128,32]{0,1:T(8,128)}, u32[]{:S(2)}) copy-start(f32[128,32]{0,1:T(8,128)} %param.2) | copy-start | bytes 49156
  37.4 1.6 %copy-start = (f32[128,256]{1,0:T(8,128)S(1)}, f32[128,256]{1,0:T(8,128)}, u32[]{:S(2)}) copy-start(f32[128,256]{1,0:T(8,128)} %get-tuple-element.5) | copy-start | bytes 393220
